TPU v7x, 32 devices: a whole 2x2x4 slice. The times are simulated.
32 devices in a mesh: fsdp: 4 (over x, core), ctx: 4 (over z), tp: 2 (over y).
Axes of the slice: x: 2, y: 2, z: 4, core: 2. Of those that a mesh axis runs over, the one named last changes fastest.
Arguments:
- tokens: bfloat16 [8192, 2048], P(('fsdp', 'ctx')), may hold values from -6 to 6
- cotangent: bfloat16 [8192, 2048], P(('fsdp', 'ctx')), may hold values from -6 to 6
- sequence_begin: int32 [8192], P('fsdp'), may hold values from 0 to 2047, as said below
- piece: int32 [8192], P('fsdp'), may hold values from 0 to 8, as said below
- padding_length: int32 [4], P('fsdp'), may hold values from 0 to 256, as said below
- attn_gain: bfloat16 [2048], P(('fsdp', 'ctx')), may hold values from 0.5 to 1.5
- q_gain: bfloat16 [128], P(('fsdp', 'ctx')), may hold values from 0.5 to 2
- k_gain: bfloat16 [128], P(('fsdp', 'ctx')), may hold values from 0.5 to 2
- w_query: bfloat16 [2048, 2048], P(('fsdp', 'ctx'), 'tp'), may hold values from -0.125 to 0.125
- key_weight: bfloat16 [2048, 1024], P(('fsdp', 'ctx'), 'tp'), may hold values from -0.125 to 0.125
- value_weight: bfloat16 [2048, 1024], P(('fsdp', 'ctx'), 'tp'), may hold values from -0.125 to 0.125
- w_out: bfloat16 [2048, 2048], P(('fsdp', 'ctx'), 'tp'), may hold values from -1 to 1
- mlp_gain: bfloat16 [2048], P(('fsdp', 'ctx')), may hold values from 0.5 to 1.5
- w_gate: bfloat16 [2048, 6144], P(('fsdp', 'ctx'), 'tp'), may hold values from -0.125 to 0.125
- w_up: bfloat16 [2048, 6144], P(('fsdp', 'ctx'), 'tp'), may hold values from -0.125 to 0.125
- w_down: bfloat16 [2048, 6144], P(('fsdp', 'ctx'), 'tp'), may hold values from -0.078125 to 0.078125
Outputs:
- layer_out: bfloat16 [8192, 2048], P(('fsdp', 'ctx'))
- grad_tokens: bfloat16 [8192, 2048], P(('fsdp', 'ctx'))
- grad_attn_gain: float32 [2048], P(('fsdp', 'ctx'))
- grad_q_gain: float32 [128], P(('fsdp', 'ctx'))
- grad_k_gain: float32 [128], P(('fsdp', 'ctx'))
- grad_query: float32 [2048, 2048], P(('fsdp', 'ctx'), 'tp')
- grad_key: float32 [2048, 1024], P(('fsdp', 'ctx'), 'tp')
- grad_value: float32 [2048, 1024], P(('fsdp', 'ctx'), 'tp')
- grad_out: float32 [2048, 2048], P(('fsdp', 'ctx'), 'tp')
- grad_mlp_gain: float32 [2048], P(('fsdp', 'ctx'))
- grad_gate: float32 [2048, 6144], P(('fsdp', 'ctx'), 'tp')
- grad_up: float32 [2048, 6144], P(('fsdp', 'ctx'), 'tp')
- grad_down: float32 [2048, 6144], P(('fsdp', 'ctx'), 'tp')
Inputs may be any that keep to these rules, and one draw needn't show every extreme that they name: `sequence_begin`: each group of 2048 tokens holds a first sequence of 1024 or more tokens from index 0, perhaps a second one after it, then its padding tokens, which form a sequence of their own; entries are indices within the group. The 256 tokens of one aligned block of 256 positions inside one sequence may form a picture piece and then share a positive number unique in the group; all other tokens are 0. `padding_length`: some group has exactly 256 padding tokens.
All inputs are finite; a program needn't handle non-finite values.
Results may differ from a plain program's by a relative error of at most 0.02.
Values may be sent and summed in bfloat16 or wider, within the bound.
A program may use at most 256 MiB of HBM per device.

v0:
```python
import jax
import jax.numpy as jnp
from jax import lax
from jax.sharding import PartitionSpec as P

HEAD_SIZE = 128
EPS = 1e-06
THETA = 1000000.0
MASK_FILL = -1e30


def rms_scale(features, gain_vec):
    inverse = lax.rsqrt(jnp.mean(features * features, axis=-1, keepdims=True) + EPS)
    return features * inverse * gain_vec


def rotate(features, cosine, sine):
    half_width = features.shape[-1] // 2
    turned = jnp.concatenate([-features[..., half_width:], features[..., :half_width]], axis=-1)
    return features * cosine + turned * sine


def rope_tables(positions, width):
    half_width = width // 2
    frequency = THETA ** (-(jnp.arange(half_width, dtype=jnp.float32) * 2.0 / width))
    angles = positions[:, None] * frequency[None, :]
    angles = jnp.concatenate([angles, angles], axis=-1)
    return (jnp.cos(angles)[:, None, :], jnp.sin(angles)[:, None, :])


def allowed(query_index, key_index, start_query, start_key, piece_query, piece_key, key_live):
    same_doc = start_query[:, None] == start_key[None, :]
    causal_pair = key_index[None, :] <= query_index[:, None]
    picture_pair = (piece_query[:, None] == piece_key[None, :]) & (piece_query[:, None] > 0)
    live_key = key_live[None, :] | (key_index[None, :] == query_index[:, None])
    return same_doc & (causal_pair | picture_pair) & live_key


def contract_last(left_side, right_side):
    return lax.dot_general(
        left_side, right_side, (((1,), (1,)), ((), ())), preferred_element_type=jnp.float32
    )


def contract_first(left_side, right_side):
    return lax.dot_general(
        left_side, right_side, (((0,), (0,)), ((), ())), preferred_element_type=jnp.float32
    )


def body(
    tokens,
    cotangent,
    sequence_begin,
    piece,
    padding_length,
    attn_gain,
    q_gain,
    k_gain,
    w_query,
    key_weight,
    value_weight,
    w_out,
    mlp_gain,
    w_gate,
    w_up,
    w_down,
):
    f32 = jnp.float32
    bf16 = jnp.bfloat16
    tok_rows = tokens.shape[0]
    group_rows = sequence_begin.shape[0]
    offset = lax.axis_index("ctx") * tok_rows
    local_index = offset + jnp.arange(tok_rows, dtype=jnp.int32)
    my_start = lax.dynamic_slice_in_dim(sequence_begin, offset, tok_rows)
    cosine, sine = rope_tables((local_index - my_start).astype(f32), HEAD_SIZE)
    key_index = jnp.arange(group_rows, dtype=jnp.int32)
    key_live = key_index < group_rows - padding_length[0]
    score_scale = HEAD_SIZE ** (-0.5)
    block_rows = min(512, group_rows)
    starts = jnp.arange(group_rows // block_rows, dtype=jnp.int32) * block_rows

    def head_prep(raw_heads, gain_vec):
        return rotate(rms_scale(raw_heads, gain_vec), cosine, sine)

    g_attn, g_query, g_key, wq_full, key_weight_whole, value_weight_whole, wo_full = (
        lax.all_gather(attn_gain, ("fsdp", "ctx"), axis=0, tiled=True),
        lax.all_gather(q_gain, ("fsdp", "ctx"), axis=0, tiled=True),
        lax.all_gather(k_gain, ("fsdp", "ctx"), axis=0, tiled=True),
        lax.all_gather(w_query, ("fsdp", "ctx"), axis=0, tiled=True),
        lax.all_gather(key_weight, ("fsdp", "ctx"), axis=0, tiled=True),
        lax.all_gather(value_weight, ("fsdp", "ctx"), axis=0, tiled=True),
        lax.all_gather(w_out, ("fsdp", "ctx"), axis=0, tiled=True),
    )
    attn_gain_f = g_attn.astype(f32)
    qgain_f = g_query.astype(f32)
    kgain_f = g_key.astype(f32)
    x_rows = tokens.astype(f32)
    normed_bf = rms_scale(x_rows, attn_gain_f).astype(bf16)
    q_raw = jnp.dot(normed_bf, wq_full, preferred_element_type=f32).reshape(tok_rows, -1, HEAD_SIZE)
    key_unrotated = jnp.dot(normed_bf, key_weight_whole, preferred_element_type=f32).reshape(
        tok_rows, -1, HEAD_SIZE
    )
    v_tok = (
        jnp.dot(normed_bf, value_weight_whole, preferred_element_type=f32)
        .astype(bf16)
        .reshape(tok_rows, -1, HEAD_SIZE)
    )
    q_tok = head_prep(q_raw, qgain_f).astype(bf16)
    k_tok = head_prep(key_unrotated, kgain_f).astype(bf16)
    q_head, k_head, v_head = (
        lax.all_to_all(q_tok, "ctx", split_axis=1, concat_axis=0, tiled=True),
        lax.all_to_all(k_tok, "ctx", split_axis=1, concat_axis=0, tiled=True),
        lax.all_to_all(v_tok, "ctx", split_axis=1, concat_axis=0, tiled=True),
    )
    kv_heads = k_head.shape[1]
    per_group = q_head.shape[1] // kv_heads
    q_group = q_head.reshape(group_rows, kv_heads, per_group, HEAD_SIZE)

    def block_scores(block_start):
        q_block = lax.dynamic_slice_in_dim(q_group, block_start, block_rows, 0)
        query_index = block_start + jnp.arange(block_rows, dtype=jnp.int32)
        pairs = allowed(
            query_index,
            key_index,
            lax.dynamic_slice_in_dim(sequence_begin, block_start, block_rows),
            sequence_begin,
            lax.dynamic_slice_in_dim(piece, block_start, block_rows),
            piece,
            key_live,
        )
        raw_scores = (
            jnp.einsum("qkrd,skd->qkrs", q_block, k_head, preferred_element_type=f32) * score_scale
        )
        return (q_block, jnp.where(pairs[:, None, None, :], raw_scores, MASK_FILL))

    def forward_block(block_start):
        q_block, scores = block_scores(block_start)
        row_max = jnp.max(scores, axis=-1, keepdims=True)
        expo_scores = jnp.exp(scores - row_max)
        row_total = jnp.sum(expo_scores, axis=-1, keepdims=True)
        prob_rows = (expo_scores / row_total).astype(bf16)
        head_out = jnp.einsum("qkrs,skd->qkrd", prob_rows, v_head, preferred_element_type=f32)
        return (
            head_out.astype(bf16).reshape(block_rows, kv_heads * per_group, HEAD_SIZE),
            (row_max + jnp.log(row_total))[..., 0],
        )

    out_blocks, lse_blocks = lax.map(forward_block, starts)
    o_head = out_blocks.reshape(group_rows, kv_heads * per_group, HEAD_SIZE)
    log_totals = lse_blocks.reshape(group_rows, kv_heads, per_group)
    o_tok = lax.all_to_all(o_head, "ctx", split_axis=0, concat_axis=1, tiled=True).reshape(
        tok_rows, -1
    )
    residual = x_rows + lax.psum(contract_last(o_tok, wo_full), "tp")
    g_mlp, wg_full, wu_full, wd_full = (
        lax.all_gather(mlp_gain, ("fsdp", "ctx"), axis=0, tiled=True),
        lax.all_gather(w_gate, ("fsdp", "ctx"), axis=0, tiled=True),
        lax.all_gather(w_up, ("fsdp", "ctx"), axis=0, tiled=True),
        lax.all_gather(w_down, ("fsdp", "ctx"), axis=0, tiled=True),
    )
    mlp_gain_f = g_mlp.astype(f32)
    normed_two = rms_scale(residual, mlp_gain_f).astype(bf16)
    gate_value = jnp.dot(normed_two, wg_full, preferred_element_type=f32)
    up_value = jnp.dot(normed_two, wu_full, preferred_element_type=f32)
    gate_sigmoid = jax.nn.sigmoid(gate_value)
    gate_silu = gate_value * gate_sigmoid
    hidden = (gate_silu * up_value).astype(bf16)
    layer_out = (
        residual
        + lax.psum(contract_last(hidden, wd_full).astype(jnp.bfloat16), "tp").astype(jnp.float32)
    ).astype(bf16)
    d_hidden = jnp.dot(cotangent, wd_full, preferred_element_type=f32)
    d_gate = (
        d_hidden * up_value * gate_sigmoid * (1.0 + gate_value * (1.0 - gate_sigmoid))
    ).astype(bf16)
    d_up = (d_hidden * gate_silu).astype(bf16)
    d_norm_two = lax.psum(contract_last(d_gate, wg_full) + contract_last(d_up, wu_full), "tp")
    _, pull_two = jax.vjp(rms_scale, residual, mlp_gain_f)
    d_residual, d_mlp_gain = pull_two(d_norm_two)
    d_residual = d_residual + cotangent.astype(f32)
    d_branch = d_residual.astype(bf16)
    d_out = (
        jnp.dot(d_branch, wo_full, preferred_element_type=f32)
        .astype(bf16)
        .reshape(tok_rows, -1, HEAD_SIZE)
    )
    d_head = lax.all_to_all(d_out, "ctx", split_axis=1, concat_axis=0, tiled=True).reshape(
        group_rows, kv_heads, per_group, HEAD_SIZE
    )

    def backward_block(accum_pair, block_start):
        key_accum, value_accum = accum_pair
        q_block, scores = block_scores(block_start)
        d_block = lax.dynamic_slice_in_dim(d_head, block_start, block_rows, 0)
        lse_block = lax.dynamic_slice_in_dim(log_totals, block_start, block_rows, 0)
        prob_rows = jnp.exp(scores - lse_block[..., None])
        d_probs = jnp.einsum("qkrd,skd->qkrs", d_block, v_head, preferred_element_type=f32)
        delta_rows = jnp.sum(prob_rows * d_probs, axis=-1, keepdims=True)
        d_scores = (prob_rows * (d_probs - delta_rows)).astype(bf16)
        d_query = (
            jnp.einsum("qkrs,skd->qkrd", d_scores, k_head, preferred_element_type=f32) * score_scale
        )
        key_accum = (
            key_accum
            + jnp.einsum("qkrs,qkrd->skd", d_scores, q_block, preferred_element_type=f32)
            * score_scale
        )
        value_accum = value_accum + jnp.einsum(
            "qkrs,qkrd->skd", prob_rows.astype(bf16), d_block, preferred_element_type=f32
        )
        return (
            (key_accum, value_accum),
            d_query.astype(bf16).reshape(block_rows, kv_heads * per_group, HEAD_SIZE),
        )

    zero_state = jnp.zeros((group_rows, kv_heads, HEAD_SIZE), f32)
    (key_accum, value_accum), dq_blocks = lax.scan(backward_block, (zero_state, zero_state), starts)
    dq_head = dq_blocks.reshape(group_rows, kv_heads * per_group, HEAD_SIZE)
    dq_tok, dk_tok, dv_tok = (
        lax.all_to_all(dq_head, "ctx", split_axis=0, concat_axis=1, tiled=True),
        lax.all_to_all(key_accum.astype(bf16), "ctx", split_axis=0, concat_axis=1, tiled=True),
        lax.all_to_all(value_accum.astype(bf16), "ctx", split_axis=0, concat_axis=1, tiled=True),
    )
    _, pull_query = jax.vjp(head_prep, q_raw, qgain_f)
    dq_raw, d_qgain = pull_query(dq_tok.astype(f32))
    _, pull_key = jax.vjp(head_prep, key_unrotated, kgain_f)
    dk_raw, d_kgain = pull_key(dk_tok.astype(f32))
    dq_flat = dq_raw.astype(bf16).reshape(tok_rows, -1)
    dk_flat = dk_raw.astype(bf16).reshape(tok_rows, -1)
    dv_flat = dv_tok.reshape(tok_rows, -1)
    d_norm_part = (
        contract_last(dq_flat, wq_full)
        + contract_last(dk_flat, key_weight_whole)
        + contract_last(dv_flat, value_weight_whole)
    )
    d_norm, d_qgain, d_kgain = lax.psum((d_norm_part, d_qgain, d_kgain), "tp")
    _, pull_one = jax.vjp(rms_scale, x_rows, attn_gain_f)
    d_tokens, d_attn_gain = pull_one(d_norm)
    grad_tokens = (d_residual + d_tokens).astype(bf16)
    all_grads = (
        lax.psum_scatter(d_attn_gain, ("fsdp", "ctx"), scatter_dimension=0, tiled=True),
        lax.psum_scatter(d_qgain, ("fsdp", "ctx"), scatter_dimension=0, tiled=True),
        lax.psum_scatter(d_kgain, ("fsdp", "ctx"), scatter_dimension=0, tiled=True),
        lax.psum_scatter(
            contract_first(normed_bf, dq_flat), ("fsdp", "ctx"), scatter_dimension=0, tiled=True
        ),
        lax.psum_scatter(
            contract_first(normed_bf, dk_flat), ("fsdp", "ctx"), scatter_dimension=0, tiled=True
        ),
        lax.psum_scatter(
            contract_first(normed_bf, dv_flat), ("fsdp", "ctx"), scatter_dimension=0, tiled=True
        ),
        lax.psum_scatter(
            contract_first(d_branch, o_tok), ("fsdp", "ctx"), scatter_dimension=0, tiled=True
        ),
        lax.psum_scatter(d_mlp_gain, ("fsdp", "ctx"), scatter_dimension=0, tiled=True),
        lax.psum_scatter(
            contract_first(normed_two, d_gate), ("fsdp", "ctx"), scatter_dimension=0, tiled=True
        ),
        lax.psum_scatter(
            contract_first(normed_two, d_up), ("fsdp", "ctx"), scatter_dimension=0, tiled=True
        ),
        lax.psum_scatter(
            contract_first(cotangent, hidden), ("fsdp", "ctx"), scatter_dimension=0, tiled=True
        ),
    )
    return (
        layer_out,
        grad_tokens,
        all_grads[0],
        all_grads[1],
        all_grads[2],
        all_grads[3],
        all_grads[4],
        all_grads[5],
        all_grads[6],
        all_grads[7],
        all_grads[8],
        all_grads[9],
        all_grads[10],
    )


def solution(mesh):
    in_specs = (
        P(("fsdp", "ctx"), None),
        P(("fsdp", "ctx"), None),
        P("fsdp"),
        P("fsdp"),
        P("fsdp"),
        P(("fsdp", "ctx")),
        P(("fsdp", "ctx")),
        P(("fsdp", "ctx")),
        P(("fsdp", "ctx"), "tp"),
        P(("fsdp", "ctx"), "tp"),
        P(("fsdp", "ctx"), "tp"),
        P(("fsdp", "ctx"), "tp"),
        P(("fsdp", "ctx")),
        P(("fsdp", "ctx"), "tp"),
        P(("fsdp", "ctx"), "tp"),
        P(("fsdp", "ctx"), "tp"),
    )
    out_specs = (
        P(("fsdp", "ctx"), None),
        P(("fsdp", "ctx"), None),
        P(("fsdp", "ctx")),
        P(("fsdp", "ctx")),
        P(("fsdp", "ctx")),
        P(("fsdp", "ctx"), "tp"),
        P(("fsdp", "ctx"), "tp"),
        P(("fsdp", "ctx"), "tp"),
        P(("fsdp", "ctx"), "tp"),
        P(("fsdp", "ctx")),
        P(("fsdp", "ctx"), "tp"),
        P(("fsdp", "ctx"), "tp"),
        P(("fsdp", "ctx"), "tp"),
    )
    return jax.shard_map(body, mesh=mesh, in_specs=in_specs, out_specs=out_specs, check_vma=False)
```

profile of v0, /device:TPU:0, one launch (start us, length us, event | category | flops | bytes accessed | tf_op | source)
XLA Modules:
  0.0 2411.7 jit_solution(119953250545401077)
XLA Ops:
  9.4 34.1 %all-gather = bf16[16,1,128]{2,1,0:T(2,128)(2,1)S(1)} all-gather(bf16[1,1,128]{2,1,0:T(2,128)(2,1)} %bitcast.402), channel_id=1, replica_groups=mesh['fsdp'=4,'ctx'=4,'tp'=2] {'fsdp','ctx'}, dimensions={0}, use_global_device_ids=true | all-gather | bytes 4352 | tf_op jit(solution)/shard_map/all_gather | solution.py:87
  47.2 29.8 %all-reduce.12 = (bf16[128]{0:T(256)(128)(2,1)S(1)}, bf16[128]{0:T(256)(128)(2,1)S(1)}) all-reduce(bf16[128]{0:T(256)(128)(2,1)S(1)} %dynamic-update-slice, bf16[128]{0:T(256)(128)(2,1)S(1)} %dynamic-update-slice.1), channel_id=1, replica_groups=mesh['fsdp'=4,'ctx'=4,'tp'=2] {'fsdp','ctx'}, use_global_device_ids=true, to_apply=%add.4 | all-reduce | flops 256 | bytes 1024
  91.1 7.5 all-gather.14.cloned.1.call-done
  102.4 46.5 %all-gather.10.cloned.1.call-done = bf16[2048,1024]{1,0:T(8,128)(2,1)} async-done(((bf16[128,1024]{1,0:T(8,128)(2,1)}), bf16[2048,1024]{1,0:T(8,128)(2,1)}) %all-gather.10.cloned.1.call-update) | async-done | bytes 4194320 | tf_op jit(solution)/shard_map/all_gather | solution.py:90
  165.8 9.7 all-to-all-done.2
  182.8 31.0 %all-to-all-done = bf16[512,8,128]{2,0,1:T(8,128)(2,1)} async-done(((bf16[512,8,128]{2,0,1:T(8,128)(2,1)}), bf16[512,8,128]{2,0,1:T(8,128)(2,1)}, u32[]{:S(2)}, u32[]{:S(2)}) %all-to-all-start) | async-done | bytes 1048608 | tf_op jit(solution)/shard_map/all_to_all | solution.py:112
  217.2 61.6 %while.30 = (s32[]{:T(128)}, bf16[4,512,2,128]{3,1,0,2:T(8,128)(2,1)}, f32[4,512,1,2]{1,3,2,0:T(2,128)S(1)}, s32[4]{0:T(128)S(1)}, s32[2048]{0:T(1024)S(1)}, /*i...) while((s32[]{:T(128)}, ...), condition=%wide.region_6.7_spmd.clone.clone, body=%wide.region_3.6_spmd.clone.clone.sunk | while | flops 1108477952 | bytes 31004356 | solution.py:149
  281.6 27.7 %all_to_all.114 = bf16[2048,2,128]{2,1,0:T(2,128)(2,1)S(1)} all-to-all(bf16[2048,2,128]{2,1,0:T(2,128)(2,1)S(1)} %copy.185), channel_id=1, replica_groups=mesh['fsdp'=4,'ctx'=4,'tp'=2] {'ctx'}, dimensions={0} | all-to-all | bytes 2097152 | tf_op jit(solution)/shard_map/all_to_all | solution.py:152
  312.7 6.9 fusion.127
  321.7 29.0 %all-gather.1 = bf16[16,1,128]{2,1,0:T(2,128)(2,1)S(1)} all-gather(bf16[1,1,128]{2,1,0:T(2,128)(2,1)S(1)} %bitcast.403), channel_id=1, replica_groups=mesh['fsdp'=4,'ctx'=4,'tp'=2] {'fsdp','ctx'}, dimensions={0}, use_global_device_ids=true | all-gather | bytes 4352 | tf_op jit(solution)/shard_map/all_gather | solution.py:157
  350.7 75.1 %all-reduce.18.cloned.1.call-done = f32[512,2048]{1,0:T(8,128)} async-done(((f32[512,2048]{1,0:T(8,128)}), f32[512,2048]{1,0:T(8,128)}) %all-reduce.18.cloned.1.call-update) | async-done | bytes 4194320 | tf_op jit(solution)/shard_map/psum | solution.py:155
  431.0 97.4 %all-gather.18.cloned.1.call-done = bf16[2048,3072]{1,0:T(8,128)(2,1)} async-done(((bf16[128,3072]{1,0:T(8,128)(2,1)}), bf16[2048,3072]{1,0:T(8,128)(2,1)}) %all-gather.18.cloned.1.call-update) | async-done | bytes 12582928 | tf_op jit(solution)/shard_map/all_gather | solution.py:158
  528.4 11.3 fusion.128
  539.7 89.7 %all-gather.20.cloned.1.call-done = bf16[2048,3072]{1,0:T(8,128)(2,1)} async-done(((bf16[128,3072]{1,0:T(8,128)(2,1)}), bf16[2048,3072]{1,0:T(8,128)(2,1)}) %all-gather.20.cloned.1.call-update) | async-done | bytes 12582928 | tf_op jit(solution)/shard_map/all_gather | solution.py:159
  629.4 12.0 fusion.129
  641.4 89.0 %all-gather.22.cloned.1.call-done = bf16[2048,3072]{1,0:T(8,128)(2,1)} async-done(((bf16[128,3072]{1,0:T(8,128)(2,1)}), bf16[2048,3072]{1,0:T(8,128)(2,1)}) %all-gather.22.cloned.1.call-update) | async-done | bytes 12582928 | tf_op jit(solution)/shard_map/all_gather | solution.py:160
  730.4 16.4 multiply_convert_fusion
  746.8 13.4 fusion.130
  760.2 12.2 convolution_add_fusion
  772.5 11.7 convolution_convert_fusion
  784.1 94.6 %all-reduce.22.cloned.1.call-done = f32[512,2048]{1,0:T(8,128)} async-done(((f32[512,2048]{1,0:T(8,128)}), f32[512,2048]{1,0:T(8,128)}) %all-reduce.22.cloned.1.call-update) | async-done | bytes 4194320 | tf_op jit(solution)/shard_map/psum | solution.py:178
  878.7 5.1 multiply_reduce_fusion
  883.9 60.6 %all-reduce.20.cloned.1.call-done = bf16[512,2048]{1,0:T(8,128)(2,1)} async-done(((bf16[512,2048]{1,0:T(8,128)(2,1)}), bf16[512,2048]{1,0:T(8,128)(2,1)}) %all-reduce.20.cloned.1.call-update) | async-done | bytes 2097168 | tf_op jit(solution)/shard_map/psum | solution.py:171
  944.5 6.0 fusion.84
  958.8 25.5 %all-to-all-done.4 = bf16[512,8,128]{2,0,1:T(8,128)(2,1)S(1)} async-done(((bf16[512,8,128]{2,0,1:T(8,128)(2,1)}), bf16[512,8,128]{2,0,1:T(8,128)(2,1)S(1)}, u32[]{:S(2)}, u32[]{:S(2)}) %all-to-all-start.4) | async-done | bytes 1048608 | tf_op jit(solution)/shard_map/all_to_all | solution.py:188
  986.5 117.5 %while.31 = (s32[]{:T(128)}, f32[2048,1,128]{0,2,1:T(8,128)S(1)}, f32[2048,1,128]{0,2,1:T(8,128)}, bf16[4,512,2,128]{3,1,0,2:T(8,128)(2,1)}, s32[4]{0:T(128)S(1)...) while((s32[]{:T(128)}, f32[2048,1,128]{0,2,1:T(8,128)S(1)}, ...), condition=%wide.region_14.15_spmd.clone.clone, body=%wide.region_12.14_spmd.clone.clone.sunk | while | flops 2726823936 | bytes 141362992 | solution.py:218
  1040.1 5.0 fusion.215
  1069.5 5.0 fusion.215
  1099.0 5.0 fusion.215
  1113.8 10.5 all-to-all-done.6
  1134.3 8.5 all-to-all-done.7
  1159.8 12.6 all-to-all-done.5
  1190.3 14.7 convolution_bitcast_fusion.1
  1214.9 7.9 fusion.102
  1224.0 5.9 fusion.115
  1230.0 14.2 fusion.133
  1244.3 14.3 fusion.134
  1259.3 35.7 %all-reduce.24.cloned.1.call-done = f32[512,2048]{1,0:T(8,128)} async-done(((f32[512,2048]{1,0:T(8,128)}), f32[512,2048]{1,0:T(8,128)}) %all-reduce.24.cloned.1.call-update) | async-done | bytes 4194320 | tf_op jit(solution)/shard_map/psum | solution.py:237
  1298.5 62.7 %all-reduce.10 = (f32[2048]{0:T(1024)S(1)}, f32[128]{0:T(128)S(1)}, f32[128]{0:T(128)S(1)}, f32[2048]{0:T(1024)S(1)}) all-reduce(f32[2048]{0:T(1024)S(1)} %get-tuple-element.391, f32[128]{0:T(128)S(1)} %get-tuple-element.393, f32[128]{0:T(128)S(1)} %get-tuple-element.395, ...), channel_id=2, replica_groups=mesh['fsdp'=4,'ctx'=4,'tp'=2] {'fsdp','ctx'}, use_global_device_ids=true, to_apply=%region_20.21.clone | all-reduce | flops 4352 | bytes 34816
  1362.0 5.4 all-reduce.11
  1368.6 5.9 fusion.86
  1374.6 167.9 %reduce-scatter.20.cloned.1.call-done = f32[128,3072]{0,1:T(8,128)} async-done(((f32[2048,3072]{0,1:T(8,128)}), f32[128,3072]{0,1:T(8,128)}) %reduce-scatter.20.cloned.1.call-update) | async-done | bytes 1572880 | tf_op jit(solution)/shard_map/reduce_scatter | solution.py:264
  1545.5 73.4 %reduce-scatter.10.cloned.1.call-done = f32[128,512]{1,0:T(8,128)} async-done(((f32[2048,512]{1,0:T(8,128)}), f32[128,512]{1,0:T(8,128)}) %reduce-scatter.10.cloned.1.call-update) | async-done | bytes 262160 | tf_op jit(solution)/shard_map/reduce_scatter | solution.py:248
  1618.9 76.2 %reduce-scatter.12.cloned.1.call-done = f32[128,512]{1,0:T(8,128)} async-done(((f32[2048,512]{1,0:T(8,128)}), f32[128,512]{1,0:T(8,128)}) %reduce-scatter.12.cloned.1.call-update) | async-done | bytes 262160 | tf_op jit(solution)/shard_map/reduce_scatter | solution.py:251
  1695.1 107.0 %reduce-scatter.14.cloned.1.call-done = f32[128,1024]{1,0:T(8,128)} async-done(((f32[2048,1024]{1,0:T(8,128)}), f32[128,1024]{1,0:T(8,128)}) %reduce-scatter.14.cloned.1.call-update) | async-done | bytes 524304 | tf_op jit(solution)/shard_map/reduce_scatter | solution.py:254
  1802.1 107.6 %reduce-scatter.8.cloned.1.call-done = f32[128,1024]{1,0:T(8,128)} async-done(((f32[2048,1024]{1,0:T(8,128)}), f32[128,1024]{1,0:T(8,128)}) %reduce-scatter.8.cloned.1.call-update) | async-done | bytes 524304 | tf_op jit(solution)/shard_map/reduce_scatter | solution.py:245
  1909.7 247.7 %reduce-scatter.16.cloned.1.call-done = f32[128,3072]{1,0:T(8,128)} async-done(((f32[2048,3072]{1,0:T(8,128)}), f32[128,3072]{1,0:T(8,128)}) %reduce-scatter.16.cloned.1.call-update) | async-done | bytes 1572880 | tf_op jit(solution)/shard_map/reduce_scatter | solution.py:258
  2157.4 247.2 %reduce-scatter.18.cloned.1.call-done = f32[128,3072]{1,0:T(8,128)} async-done(((f32[2048,3072]{1,0:T(8,128)}), f32[128,3072]{1,0:T(8,128)}) %reduce-scatter.18.cloned.1.call-update) | async-done | bytes 1572880 | tf_op jit(solution)/shard_map/reduce_scatter | solution.py:261
  (343 shorter events, 295.2 us)
Async XLA Ops:
  7.2 75.3 %copy-start.2 = (bf16[512,2048]{1,0:T(8,128)(2,1)S(1)}, bf16[512,2048]{1,0:T(8,128)(2,1)}, u32[]{:S(2)}) copy-start(bf16[512,2048]{1,0:T(8,128)(2,1)} %param.20) | copy-start | bytes 6291460
  7.2 75.3 %all-gather.12.cloned.1.call-start = ((), (), s32[]{:S(2)}) async-start(), calls=%async_computation.16 | async-start | bytes 2228224 | tf_op jit(solution)/shard_map/all_gather | solution.py:91
  7.9 90.8 %all-gather.14.cloned.1.call-start = ((), (), s32[]{:S(2)}) async-start(), calls=%async_computation.17 | async-start | bytes 2228224 | tf_op jit(solution)/shard_map/all_gather | solution.py:92
  8.7 140.3 %all-gather.10.cloned.1.call-start = ((), (), s32[]{:S(2)}) async-start(), calls=%async_computation.15 | async-start | bytes 4456448 | tf_op jit(solution)/shard_map/all_gather | solution.py:90
  43.5 105.5 %copy-start.29 = (f32[16,1,128]{2,1,0:T(1,128)}, f32[16,1,128]{2,1,0:T(1,128)S(1)}, u32[]{:S(2)}) copy-start(f32[16,1,128]{2,1,0:T(1,128)S(1)} %convert_element_type.182) | copy-start | bytes 24580
  77.1 85.8 %copy-start.44 = (f32[128]{0:T(128)}, f32[128]{0:T(128)S(1)}, u32[]{:S(2)}) copy-start(f32[128]{0:T(128)S(1)} %convert_element_type.135) | copy-start | bytes 1540
  77.1 9.0 copy-start.46
  79.1 83.8 %copy-start.12 = (f32[512,128]{1,0:T(8,128)}, f32[512,128]{1,0:T(8,128)S(1)}, u32[]{:S(2)}) copy-start(f32[512,128]{1,0:T(8,128)S(1)} %get-tuple-element.476) | copy-start | bytes 786436
  79.1 83.8 %copy-start.14 = (f32[512,128]{1,0:T(8,128)}, f32[512,128]{1,0:T(8,128)S(1)}, u32[]{:S(2)}) copy-start(f32[512,128]{1,0:T(8,128)S(1)} %get-tuple-element.477) | copy-start | bytes 786436
  82.5 66.5 %copy-start.37 = (f32[512]{0:T(512)}, f32[512]{0:T(512)S(1)}, u32[]{:S(2)}) copy-start(f32[512]{0:T(512)S(1)} %fusion.109) | copy-start | bytes 6148
  87.7 68.4 %all-to-all-start.1 = ((bf16[512,4,128]{0,2,1:T(8,128)(2,1)}), bf16[512,4,128]{0,2,1:T(8,128)(2,1)S(1)}, u32[]{:S(2)}, u32[]{:S(2)}) async-start(bf16[512,4,128]{0,2,1:T(8,128)(2,1)} %fusion.99), calls=%async_computation.1 | async-start | bytes 1048576 | tf_op jit(solution)/shard_map/all_to_all | solution.py:113
  156.1 19.4 all-to-all-start.2
  165.8 51.4 %copy-start.25 = (s32[2048]{0:T(1024)S(1)}, s32[2048]{0:T(1024)}, u32[]{:S(2)}) copy-start(s32[2048]{0:T(1024)} %param.22) | copy-start | bytes 24580
  165.8 51.4 %copy-start.26 = (s32[2048]{0:T(1024)S(1)}, s32[2048]{0:T(1024)}, u32[]{:S(2)}) copy-start(s32[2048]{0:T(1024)} %param.23) | copy-start | bytes 24580
  175.5 38.3 %all-to-all-start = ((bf16[512,8,128]{2,0,1:T(8,128)(2,1)}), bf16[512,8,128]{2,0,1:T(8,128)(2,1)}, u32[]{:S(2)}, u32[]{:S(2)}) async-start(bf16[512,8,128]{2,0,1:T(8,128)(2,1)} %fusion.92), calls=%async_computation | async-start | bytes 2097152 | tf_op jit(solution)/shard_map/all_to_all | solution.py:112
  179.7 132.9 %all-gather.16.cloned.1.call-start = ((), (), s32[]{:S(2)}) async-start(), calls=%async_computation.18 | async-start | bytes 4456448 | tf_op jit(solution)/shard_map/all_gather | solution.py:93
  180.3 245.5 %all-reduce.18.cloned.1.call-start = ((), (), s32[]{:S(2)}) async-start(), calls=%async_computation.19 | async-start | bytes 8388608 | tf_op jit(solution)/shard_map/psum | solution.py:155
  319.6 208.8 %all-gather.18.cloned.1.call-start = ((), (), s32[]{:S(2)}) async-start(), calls=%async_computation.20 | async-start | bytes 13369344 | tf_op jit(solution)/shard_map/all_gather | solution.py:158
  320.2 309.3 %all-gather.20.cloned.1.call-start = ((), (), s32[]{:S(2)}) async-start(), calls=%async_computation.21 | async-start | bytes 13369344 | tf_op jit(solution)/shard_map/all_gather | solution.py:159
  320.9 409.5 %all-gather.22.cloned.1.call-start = ((), (), s32[]{:S(2)}) async-start(), calls=%async_computation.22 | async-start | bytes 13369344 | tf_op jit(solution)/shard_map/all_gather | solution.py:160
  321.7 557.1 %all-reduce.22.cloned.1.call-start = ((), (), s32[]{:S(2)}) async-start(), calls=%async_computation.24 | async-start | bytes 8388608 | tf_op jit(solution)/shard_map/psum | solution.py:178
  431.0 97.4 %copy-start.22 = (bf16[512,2048]{1,0:T(8,128)(2,1)}, bf16[512,2048]{1,0:T(8,128)(2,1)S(1)}, u32[]{:S(2)}) copy-start(bf16[512,2048]{1,0:T(8,128)(2,1)S(1)} %multiply_convert_fusion.3) | copy-start | bytes 6291460
  539.7 190.8 %copy-start.20 = (bf16[512,2048]{1,0:T(8,128)(2,1)S(1)}, bf16[512,2048]{1,0:T(8,128)(2,1)}, u32[]{:S(2)}) copy-start(bf16[512,2048]{1,0:T(8,128)(2,1)} %param.21) | copy-start | bytes 6291460
  746.8 13.4 copy-start.51
  746.8 13.4 copy-start.50
  772.4 172.0 %all-reduce.20.cloned.1.call-start = ((), (), s32[]{:S(2)}) async-start(), calls=%async_computation.23 | async-start | bytes 4194304 | tf_op jit(solution)/shard_map/psum | solution.py:171
  954.0 30.3 %all-to-all-start.4 = ((bf16[512,8,128]{2,0,1:T(8,128)(2,1)}), bf16[512,8,128]{2,0,1:T(8,128)(2,1)S(1)}, u32[]{:S(2)}, u32[]{:S(2)}) async-start(bf16[512,8,128]{2,0,1:T(8,128)(2,1)} %bitcast.303), calls=%async_computation.4 | async-start | bytes 2097152 | tf_op jit(solution)/shard_map/all_to_all | solution.py:188
  1003.1 7.9 copy-start.1
  1032.2 7.9 copy-start.1
  1061.6 7.9 copy-start.1
  1091.1 7.9 copy-start.1
  1106.8 17.5 all-to-all-start.6
  1124.3 18.5 all-to-all-start.7
  1142.8 29.6 %all-to-all-start.5 = ((bf16[2048,2,128]{2,1,0:T(2,128)(2,1)}), bf16[2048,2,128]{2,1,0:T(2,128)(2,1)}, u32[]{:S(2)}, u32[]{:S(2)}) async-start(bf16[2048,2,128]{2,1,0:T(2,128)(2,1)} %copy.191), calls=%async_computation.5 | async-start | bytes 2097152 | tf_op jit(solution)/shard_map/all_to_all | solution.py:221
  1147.0 7.9 copy-start.11
  1147.0 7.9 copy-start.18
  1147.1 7.9 copy-start.34
  1147.1 7.9 copy-start.47
  1147.1 147.9 %all-reduce.24.cloned.1.call-start = ((), (), s32[]{:S(2)}) async-start(), calls=%async_computation.25 | async-start | bytes 8388608 | tf_op jit(solution)/shard_map/psum | solution.py:237
  1188.8 353.7 %reduce-scatter.20.cloned.1.call-start = ((), (), s32[]{:S(2)}) async-start(), calls=%async_computation.32 | async-start | bytes 26738688 | tf_op jit(solution)/shard_map/reduce_scatter | solution.py:264
  1205.0 413.9 %reduce-scatter.10.cloned.1.call-start = ((), (), s32[]{:S(2)}) async-start(), calls=%async_computation.27 | async-start | bytes 4456448 | tf_op jit(solution)/shard_map/reduce_scatter | solution.py:248
  1210.1 485.0 %reduce-scatter.12.cloned.1.call-start = ((), (), s32[]{:S(2)}) async-start(), calls=%async_computation.28 | async-start | bytes 4456448 | tf_op jit(solution)/shard_map/reduce_scatter | solution.py:251
  1213.7 588.4 %reduce-scatter.14.cloned.1.call-start = ((), (), s32[]{:S(2)}) async-start(), calls=%async_computation.29 | async-start | bytes 8912896 | tf_op jit(solution)/shard_map/reduce_scatter | solution.py:254
  1222.8 686.9 %reduce-scatter.8.cloned.1.call-start = ((), (), s32[]{:S(2)}) async-start(), calls=%async_computation.26 | async-start | bytes 8912896 | tf_op jit(solution)/shard_map/reduce_scatter | solution.py:245
  1230.0 927.5 %reduce-scatter.16.cloned.1.call-start = ((), (), s32[]{:S(2)}) async-start(), calls=%async_computation.30 | async-start | bytes 26738688 | tf_op jit(solution)/shard_map/reduce_scatter | solution.py:258
  1244.2 1160.4 %reduce-scatter.18.cloned.1.call-start = ((), (), s32[]{:S(2)}) async-start(), calls=%async_computation.31 | async-start | bytes 26738688 | tf_op jit(solution)/shard_map/reduce_scatter | solution.py:261
  1258.6 39.9 %copy-start.41 = (f32[2048]{0:T(1024)S(1)}, f32[2048]{0:T(1024)}, u32[]{:S(2)}) copy-start(f32[2048]{0:T(1024)} %get-tuple-element.389) | copy-start | bytes 24580
  1258.6 110.0 %copy-start.43 = (f32[512]{0:T(512)S(1)}, f32[512]{0:T(512)}, u32[]{:S(2)}) copy-start(f32[512]{0:T(512)} %copy-done.42) | copy-start | bytes 6148
  (35 other events, 100.2 us)
Sparse Core Ops, SparseCore 0:
  10.2 44.3 all-gather.11
  56.8 41.7 all-gather.13
  100.9 47.9 all-gather.9
  182.4 57.7 all-gather.15
  319.7 106.0 all-reduce.17
  427.9 100.4 all-gather.17
  530.7 98.6 all-gather.19
  631.7 98.6 all-gather.21
  772.5 106.1 all-reduce.21
  881.5 62.9 all-reduce.19
  1188.9 106.0 all-reduce.23
  1298.9 243.5 reduce-scatter.19
  1546.9 71.9 reduce-scatter.9
  1623.2 71.8 reduce-scatter.11
  1699.6 102.4 reduce-scatter.13
  1806.5 103.1 reduce-scatter.7
  1914.2 243.1 reduce-scatter.15
  2162.0 242.6 reduce-scatter.17
where the time goes:
time: 2420 us; the launch traced here: 2410 us
  waiting for transfers between devices  1730 us (71%)
  matrix products  276 us (11%)
  blocking collectives  189 us (8%)
  other arithmetic  103 us (4%)
  local copies, waits for them, and re-layouts  55.2 us (2%)
  starting transfers between devices  29.6 us (1%)
    reduce_scatter x1, waiting for transfers between devices, body(): lax.psum_scatter(contract_first(normed_two, d_gate), ('fsdp', 'ctx'), sca...  248 us
    reduce_scatter x1, waiting for transfers between devices, body(): lax.psum_scatter(contract_first(normed_two, d_up), ('fsdp', 'ctx'), scatt...  247 us
    reduce_scatter x1, waiting for transfers between devices, body(): lax.psum_scatter(contract_first(cotangent, hidden), ('fsdp', 'ctx'), scat...  168 us
    reduce_scatter x1, waiting for transfers between devices, body(): lax.psum_scatter(contract_first(normed_bf, dq_flat), ('fsdp', 'ctx'), sca...  108 us
    reduce_scatter x1, waiting for transfers between devices, body(): lax.psum_scatter(contract_first(d_branch, o_tok), ('fsdp', 'ctx'), scatte...  107 us
    all_gather x1, waiting for transfers between devices, body(): lax.all_gather(w_gate, ('fsdp', 'ctx'), axis=0, tiled=True)  97.4 us
    psum x1, waiting for transfers between devices, body(): lax.psum(contract_last(d_gate, wg_full) + contract_last(d_up, wu_full), '...  94.6 us
    unnamed x2, blocking collectives  92.6 us
  transfers between devices with their start and end apart: 25, of which 22 were waited for; matrix products, arithmetic and copies ran while one was open for 10% of the time, Pallas kernels for 0%

commit v1 on v0

--- a/solution.py
+++ b/solution.py
@@ -7,6 +7,18 @@
 EPS = 1e-06
 THETA = 1000000.0
 MASK_FILL = -1e30
+
+
+def gather_by_bits(x, axis, dim):
+    ways, here, step = (lax.axis_size(axis), lax.axis_index(axis), x.shape[dim])
+    line, have = (x, 1)
+    while have < ways:
+        line = jnp.concatenate(
+            [line, lax.ppermute(line, axis, [(d, (d - have) % ways) for d in range(ways)])],
+            axis=dim,
+        )
+        have = 2 * have
+    return jnp.roll(line, here * step, axis=dim)
 
 
 def rms_scale(features, gain_vec):
@@ -155,7 +167,7 @@
     residual = x_rows + lax.psum(contract_last(o_tok, wo_full), "tp")
     g_mlp, wg_full, wu_full, wd_full = (
         lax.all_gather(mlp_gain, ("fsdp", "ctx"), axis=0, tiled=True),
-        lax.all_gather(w_gate, ("fsdp", "ctx"), axis=0, tiled=True),
+        gather_by_bits(w_gate, ("fsdp", "ctx"), 0),
         lax.all_gather(w_up, ("fsdp", "ctx"), axis=0, tiled=True),
         lax.all_gather(w_down, ("fsdp", "ctx"), axis=0, tiled=True),
     )

time: 2420 us -> 2410 us (level)
  waiting for transfers between devices: 1730 us -> 1660 us
  local copies, waits for them, and re-layouts: 55.2 us -> 83.2 us
    ppermute x0 -> x4, waiting for transfers between devices: none -> 287 us  [gather_by_bits(): lax.ppermute(line, axis, [(d, (d - have) % ways) for d in range(ways)])]
    all_gather x1 -> x0, waiting for transfers between devices: 97.4 us -> none  [body(): lax.all_gather(w_gate, ('fsdp', 'ctx'), axis=0, tiled=True)]
    all_gather x1, waiting for transfers between devices: 89.7 us -> 0.01 us  [body(): lax.all_gather(w_up, ('fsdp', 'ctx'), axis=0, tiled=True)]
    all_gather x1, waiting for transfers between devices: 89 us -> 0.01 us  [body(): lax.all_gather(w_down, ('fsdp', 'ctx'), axis=0, tiled=True)]
    psum x1, waiting for transfers between devices: 75.1 us -> 0.01 us  [body(): residual = x_rows + lax.psum(contract_last(o_tok, wo_full), 'tp')]
  transfers between devices with their start and end apart: 25 -> 28, of which waited for: 22 -> 22; matrix products, arithmetic and copies ran while one was open for 10% -> 11% of each run, Pallas kernels for 0% -> 0%
where the time goes in v1:
time: 2410 us; the launch traced here: 2400 us
  waiting for transfers between devices  1660 us (69%)
  matrix products  277 us (11%)
  blocking collectives  203 us (8%)
  other arithmetic  111 us (5%)
  local copies, waits for them, and re-layouts  83.2 us (3%)
  starting transfers between devices  31.6 us (1%)
    ppermute x4, waiting for transfers between devices, gather_by_bits(): lax.ppermute(line, axis, [(d, (d - have) % ways) for d in range(ways)])  287 us
    reduce_scatter x1, waiting for transfers between devices, body(): lax.psum_scatter(contract_first(normed_two, d_gate), ('fsdp', 'ctx'), sca...  248 us
    reduce_scatter x1, waiting for transfers between devices, body(): lax.psum_scatter(contract_first(normed_two, d_up), ('fsdp', 'ctx'), scatt...  247 us
    reduce_scatter x1, waiting for transfers between devices, body(): lax.psum_scatter(contract_first(cotangent, hidden), ('fsdp', 'ctx'), scat...  168 us
    reduce_scatter x1, waiting for transfers between devices, body(): lax.psum_scatter(contract_first(normed_bf, dq_flat), ('fsdp', 'ctx'), sca...  108 us
    reduce_scatter x1, waiting for transfers between devices, body(): lax.psum_scatter(contract_first(d_branch, o_tok), ('fsdp', 'ctx'), scatte...  107 us
    psum x1, waiting for transfers between devices, body(): lax.psum(contract_last(d_gate, wg_full) + contract_last(d_up, wu_full), '...  97.5 us
    unnamed x2, blocking collectives  92.6 us
  transfers between devices with their start and end apart: 28, of which 22 were waited for; matrix products, arithmetic and copies ran while one was open for 11% of the time, Pallas kernels for 0%

profile of v1, /device:TPU:0, one launch (start us, length us, event | category | flops | bytes accessed | tf_op | source)
XLA Modules:
  0.0 2403.7 jit_solution(6254500835759103741)
XLA Ops:
  9.4 34.1 %all-gather = bf16[16,1,128]{2,1,0:T(2,128)(2,1)S(1)} all-gather(bf16[1,1,128]{2,1,0:T(2,128)(2,1)} %bitcast.400), channel_id=1, replica_groups=mesh['fsdp'=4,'ctx'=4,'tp'=2] {'fsdp','ctx'}, dimensions={0}, use_global_device_ids=true | all-gather | bytes 4352 | tf_op jit(solution)/shard_map/all_gather | solution.py:99
  47.2 29.8 %all-reduce.12 = (bf16[128]{0:T(256)(128)(2,1)S(1)}, bf16[128]{0:T(256)(128)(2,1)S(1)}) all-reduce(bf16[128]{0:T(256)(128)(2,1)S(1)} %dynamic-update-slice, bf16[128]{0:T(256)(128)(2,1)S(1)} %dynamic-update-slice.1), channel_id=1, replica_groups=mesh['fsdp'=4,'ctx'=4,'tp'=2] {'fsdp','ctx'}, use_global_device_ids=true, to_apply=%add.4 | all-reduce | flops 256 | bytes 1024
  91.1 7.6 all-gather.13.cloned.1.call-done
  102.4 46.5 %all-gather.9.cloned.1.call-done = bf16[2048,1024]{1,0:T(8,128)(2,1)} async-done(((bf16[128,1024]{1,0:T(8,128)(2,1)}), bf16[2048,1024]{1,0:T(8,128)(2,1)}) %all-gather.9.cloned.1.call-update) | async-done | bytes 4194320 | tf_op jit(solution)/shard_map/all_gather | solution.py:102
  165.8 9.7 all-to-all-done.2
  182.9 30.9 %all-to-all-done = bf16[512,8,128]{2,0,1:T(8,128)(2,1)} async-done(((bf16[512,8,128]{2,0,1:T(8,128)(2,1)}), bf16[512,8,128]{2,0,1:T(8,128)(2,1)}, u32[]{:S(2)}, u32[]{:S(2)}) %all-to-all-start) | async-done | bytes 1048608 | tf_op jit(solution)/shard_map/all_to_all | solution.py:124
  217.1 63.7 %while.30 = (s32[]{:T(128)}, bf16[4,512,2,128]{3,1,0,2:T(8,128)(2,1)}, f32[4,512,1,2]{1,3,2,0:T(2,128)}, s32[4]{0:T(128)S(1)}, s32[2048]{0:T(1024)S(1)}, /*index...) while((s32[]{:T(128)}, ...), condition=%wide.region_6.7_spmd.clone.clone, body=%wide.region_3.6_spmd.clone.clone.sunk | while | flops 1108477952 | bytes 31004864 | solution.py:161
  284.1 27.7 %all_to_all.114 = bf16[2048,2,128]{2,1,0:T(2,128)(2,1)S(1)} all-to-all(bf16[2048,2,128]{2,1,0:T(2,128)(2,1)S(1)} %copy.185), channel_id=1, replica_groups=mesh['fsdp'=4,'ctx'=4,'tp'=2] {'ctx'}, dimensions={0} | all-to-all | bytes 2097152 | tf_op jit(solution)/shard_map/all_to_all | solution.py:164
  315.2 7.0 fusion.136
  324.1 17.7 collective-permute-done
  341.9 71.3 %collective-permute-done.1 = bf16[256,3072]{1,0:T(8,128)(2,1)S(1)} collective-permute-done((bf16[256,3072]{1,0:T(8,128)(2,1)S(1)}, bf16[256,3072]{1,0:T(8,128)(2,1)S(1)}, u32[]{:S(2)}, u32[]{:S(2)}) %collective-permute-start.1) | collective-permute-done | bytes 1572896 | tf_op jit(solution)/shard_map/ppermute | solution.py:17
  413.5 43.2 %collective-permute-done.2 = bf16[512,3072]{1,0:T(8,128)(2,1)S(1)} collective-permute-done((bf16[512,3072]{1,0:T(8,128)(2,1)S(1)}, bf16[512,3072]{1,0:T(8,128)(2,1)S(1)}, u32[]{:S(2)}, u32[]{:S(2)}) %collective-permute-start.2) | collective-permute-done | bytes 3145760 | tf_op jit(solution)/shard_map/ppermute | solution.py:17
  461.5 43.2 %all-gather.1 = bf16[16,1,128]{2,1,0:T(2,128)(2,1)S(1)} all-gather(bf16[1,1,128]{2,1,0:T(2,128)(2,1)S(1)} %bitcast.401), channel_id=1, replica_groups=mesh['fsdp'=4,'ctx'=4,'tp'=2] {'fsdp','ctx'}, dimensions={0}, use_global_device_ids=true | all-gather | bytes 4352 | tf_op jit(solution)/shard_map/all_gather | solution.py:169
  512.5 154.7 %collective-permute-done.3 = bf16[1024,3072]{1,0:T(8,128)(2,1)} collective-permute-done((bf16[1024,3072]{1,0:T(8,128)(2,1)}, bf16[1024,3072]{1,0:T(8,128)(2,1)}, u32[]{:S(2)}, u32[]{:S(2)}) %collective-permute-start.3) | collective-permute-done | bytes 6291488 | tf_op jit(solution)/shard_map/ppermute | solution.py:17
  667.2 5.9 constant_dynamic-update-slice_fusion.5
  678.2 5.9 constant_dynamic-update-slice_fusion
  690.6 12.3 fusion.137
  702.9 11.5 fusion.138
  714.4 17.5 multiply_convert_fusion.1
  731.9 12.1 fusion.139
  744.1 14.2 fusion.93
  758.3 11.6 convolution_convert_fusion
  769.9 97.5 %all-reduce.22.cloned.1.call-done = f32[512,2048]{1,0:T(8,128)} async-done(((f32[512,2048]{1,0:T(8,128)}), f32[512,2048]{1,0:T(8,128)}) %all-reduce.22.cloned.1.call-update) | async-done | bytes 4194320 | tf_op jit(solution)/shard_map/psum | solution.py:190
  867.4 5.1 multiply_reduce_fusion
  872.5 60.8 %all-reduce.20.cloned.1.call-done = bf16[512,2048]{1,0:T(8,128)(2,1)} async-done(((bf16[512,2048]{1,0:T(8,128)(2,1)}), bf16[512,2048]{1,0:T(8,128)(2,1)}) %all-reduce.20.cloned.1.call-update) | async-done | bytes 2097168 | tf_op jit(solution)/shard_map/psum | solution.py:183
  933.3 6.0 fusion.88
  947.9 25.5 %all-to-all-done.4 = bf16[512,8,128]{2,0,1:T(8,128)(2,1)S(1)} async-done(((bf16[512,8,128]{2,0,1:T(8,128)(2,1)}), bf16[512,8,128]{2,0,1:T(8,128)(2,1)S(1)}, u32[]{:S(2)}, u32[]{:S(2)}) %all-to-all-start.4) | async-done | bytes 1048608 | tf_op jit(solution)/shard_map/all_to_all | solution.py:200
  975.6 120.5 %while.31 = (s32[]{:T(128)}, f32[2048,1,128]{0,2,1:T(8,128)S(1)}, f32[2048,1,128]{0,2,1:T(8,128)}, bf16[4,512,2,128]{3,1,0,2:T(8,128)(2,1)}, s32[4]{0:T(128)S(1)...) while((s32[]{:T(128)}, f32[2048,1,128]{0,2,1:T(8,128)S(1)}, ...), condition=%wide.region_14.15_spmd.clone.clone, body=%wide.region_12.14_spmd.clone.clone.sunk | while | flops 2726823936 | bytes 141362992 | solution.py:230
  1091.1 5.0 fusion.222
  1105.9 10.5 all-to-all-done.6
  1126.4 8.5 all-to-all-done.7
  1151.9 12.5 all-to-all-done.5
  1182.4 14.2 convolution_bitcast_fusion.1
  1206.4 7.9 fusion.109
  1215.6 6.0 fusion.124
  1221.6 14.3 fusion.142
  1235.9 14.2 fusion.143
  1250.8 36.2 %all-reduce.24.cloned.1.call-done = f32[512,2048]{1,0:T(8,128)} async-done(((f32[512,2048]{1,0:T(8,128)}), f32[512,2048]{1,0:T(8,128)}) %all-reduce.24.cloned.1.call-update) | async-done | bytes 4194320 | tf_op jit(solution)/shard_map/psum | solution.py:249
  1290.5 62.8 %all-reduce.10 = (f32[2048]{0:T(1024)S(1)}, f32[128]{0:T(128)S(1)}, f32[128]{0:T(128)S(1)}, f32[2048]{0:T(1024)S(1)}) all-reduce(f32[2048]{0:T(1024)S(1)} %get-tuple-element.391, f32[128]{0:T(128)S(1)} %get-tuple-element.393, f32[128]{0:T(128)S(1)} %get-tuple-element.395, ...), channel_id=2, replica_groups=mesh['fsdp'=4,'ctx'=4,'tp'=2] {'fsdp','ctx'}, use_global_device_ids=true, to_apply=%region_20.21.clone | all-reduce | flops 4352 | bytes 34816
  1354.1 5.4 all-reduce.11
  1360.7 5.9 fusion.90
  1366.7 168.0 %reduce-scatter.20.cloned.1.call-done = f32[128,3072]{0,1:T(8,128)} async-done(((f32[2048,3072]{0,1:T(8,128)}), f32[128,3072]{0,1:T(8,128)}) %reduce-scatter.20.cloned.1.call-update) | async-done | bytes 1572880 | tf_op jit(solution)/shard_map/reduce_scatter | solution.py:276
  1537.7 73.2 %reduce-scatter.10.cloned.1.call-done = f32[128,512]{1,0:T(8,128)} async-done(((f32[2048,512]{1,0:T(8,128)}), f32[128,512]{1,0:T(8,128)}) %reduce-scatter.10.cloned.1.call-update) | async-done | bytes 262160 | tf_op jit(solution)/shard_map/reduce_scatter | solution.py:260
  1610.8 76.3 %reduce-scatter.12.cloned.1.call-done = f32[128,512]{1,0:T(8,128)} async-done(((f32[2048,512]{1,0:T(8,128)}), f32[128,512]{1,0:T(8,128)}) %reduce-scatter.12.cloned.1.call-update) | async-done | bytes 262160 | tf_op jit(solution)/shard_map/reduce_scatter | solution.py:263
  1687.2 107.0 %reduce-scatter.14.cloned.1.call-done = f32[128,1024]{1,0:T(8,128)} async-done(((f32[2048,1024]{1,0:T(8,128)}), f32[128,1024]{1,0:T(8,128)}) %reduce-scatter.14.cloned.1.call-update) | async-done | bytes 524304 | tf_op jit(solution)/shard_map/reduce_scatter | solution.py:266
  1794.2 107.6 %reduce-scatter.8.cloned.1.call-done = f32[128,1024]{1,0:T(8,128)} async-done(((f32[2048,1024]{1,0:T(8,128)}), f32[128,1024]{1,0:T(8,128)}) %reduce-scatter.8.cloned.1.call-update) | async-done | bytes 524304 | tf_op jit(solution)/shard_map/reduce_scatter | solution.py:257
  1901.8 247.7 %reduce-scatter.16.cloned.1.call-done = f32[128,3072]{1,0:T(8,128)} async-done(((f32[2048,3072]{1,0:T(8,128)}), f32[128,3072]{1,0:T(8,128)}) %reduce-scatter.16.cloned.1.call-update) | async-done | bytes 1572880 | tf_op jit(solution)/shard_map/reduce_scatter | solution.py:270
  2149.5 247.2 %reduce-scatter.18.cloned.1.call-done = f32[128,3072]{1,0:T(8,128)} async-done(((f32[2048,3072]{1,0:T(8,128)}), f32[128,3072]{1,0:T(8,128)}) %reduce-scatter.18.cloned.1.call-update) | async-done | bytes 1572880 | tf_op jit(solution)/shard_map/reduce_scatter | solution.py:273
  (389 shorter events, 330.2 us)
Async XLA Ops:
  7.2 75.3 %copy-start.2 = (bf16[512,2048]{1,0:T(8,128)(2,1)S(1)}, bf16[512,2048]{1,0:T(8,128)(2,1)}, u32[]{:S(2)}) copy-start(bf16[512,2048]{1,0:T(8,128)(2,1)} %param.20) | copy-start | bytes 6291460
  7.2 75.3 %all-gather.11.cloned.1.call-start = ((), (), s32[]{:S(2)}) async-start(), calls=%async_computation.16 | async-start | bytes 2228224 | tf_op jit(solution)/shard_map/all_gather | solution.py:103
  7.9 90.8 %all-gather.13.cloned.1.call-start = ((), (), s32[]{:S(2)}) async-start(), calls=%async_computation.17 | async-start | bytes 2228224 | tf_op jit(solution)/shard_map/all_gather | solution.py:104
  8.7 140.3 %all-gather.9.cloned.1.call-start = ((), (), s32[]{:S(2)}) async-start(), calls=%async_computation.15 | async-start | bytes 4456448 | tf_op jit(solution)/shard_map/all_gather | solution.py:102
  43.5 105.4 %copy-start.42 = (f32[16,1,128]{2,1,0:T(1,128)}, f32[16,1,128]{2,1,0:T(1,128)S(1)}, u32[]{:S(2)}) copy-start(f32[16,1,128]{2,1,0:T(1,128)S(1)} %convert_element_type.182) | copy-start | bytes 24580
  77.1 85.8 %copy-start.57 = (f32[128]{0:T(128)}, f32[128]{0:T(128)S(1)}, u32[]{:S(2)}) copy-start(f32[128]{0:T(128)S(1)} %convert_element_type.135) | copy-start | bytes 1540
  79.1 83.8 %copy-start.23 = (f32[512,128]{1,0:T(8,128)}, f32[512,128]{1,0:T(8,128)S(1)}, u32[]{:S(2)}) copy-start(f32[512,128]{1,0:T(8,128)S(1)} %get-tuple-element.476) | copy-start | bytes 786436
  79.1 83.8 %copy-start.25 = (f32[512,128]{1,0:T(8,128)}, f32[512,128]{1,0:T(8,128)S(1)}, u32[]{:S(2)}) copy-start(f32[512,128]{1,0:T(8,128)S(1)} %get-tuple-element.477) | copy-start | bytes 786436
  82.5 66.5 %copy-start.50 = (f32[512]{0:T(512)}, f32[512]{0:T(512)S(1)}, u32[]{:S(2)}) copy-start(f32[512]{0:T(512)S(1)} %fusion.116) | copy-start | bytes 6148
  87.6 68.4 %all-to-all-start.1 = ((bf16[512,4,128]{0,2,1:T(8,128)(2,1)}), bf16[512,4,128]{0,2,1:T(8,128)(2,1)S(1)}, u32[]{:S(2)}, u32[]{:S(2)}) async-start(bf16[512,4,128]{0,2,1:T(8,128)(2,1)} %fusion.106), calls=%async_computation.1 | async-start | bytes 1048576 | tf_op jit(solution)/shard_map/all_to_all | solution.py:125
  156.0 19.4 all-to-all-start.2
  165.8 51.4 %copy-start.36 = (s32[2048]{0:T(1024)S(1)}, s32[2048]{0:T(1024)}, u32[]{:S(2)}) copy-start(s32[2048]{0:T(1024)} %param.22) | copy-start | bytes 24580
  165.8 51.4 %copy-start.38 = (s32[2048]{0:T(1024)S(1)}, s32[2048]{0:T(1024)}, u32[]{:S(2)}) copy-start(s32[2048]{0:T(1024)} %param.23) | copy-start | bytes 24580
  175.4 38.3 %all-to-all-start = ((bf16[512,8,128]{2,0,1:T(8,128)(2,1)}), bf16[512,8,128]{2,0,1:T(8,128)(2,1)}, u32[]{:S(2)}, u32[]{:S(2)}) async-start(bf16[512,8,128]{2,0,1:T(8,128)(2,1)} %fusion.99), calls=%async_computation | async-start | bytes 2097152 | tf_op jit(solution)/shard_map/all_to_all | solution.py:124
  179.7 135.5 %all-gather.15.cloned.1.call-start = ((), (), s32[]{:S(2)}) async-start(), calls=%async_computation.18 | async-start | bytes 4456448 | tf_op jit(solution)/shard_map/all_gather | solution.py:105
  180.3 503.8 %all-reduce.18.cloned.1.call-start = ((), (), s32[]{:S(2)}) async-start(), calls=%async_computation.19 | async-start | bytes 8388608 | tf_op jit(solution)/shard_map/psum | solution.py:167
  280.8 34.3 %copy-start.19 = (bf16[2048,1,128]{2,0,1:T(8,128)(2,1)}, bf16[2048,1,128]{2,0,1:T(8,128)(2,1)S(1)}, u32[]{:S(2)}) copy-start(bf16[2048,1,128]{2,0,1:T(8,128)(2,1)S(1)} %get-tuple-element.758) | copy-start | bytes 1572868
  280.8 34.3 %copy-start.21 = (bf16[2048,1,128]{2,0,1:T(8,128)(2,1)}, bf16[2048,1,128]{2,0,1:T(8,128)(2,1)S(1)}, u32[]{:S(2)}) copy-start(bf16[2048,1,128]{2,0,1:T(8,128)(2,1)S(1)} %get-tuple-element.759) | copy-start | bytes 1572868
  280.8 34.3 %copy-start.63 = (s32[4]{0:T(128)}, s32[4]{0:T(128)S(1)}, u32[]{:S(2)}) copy-start(s32[4]{0:T(128)S(1)} %get-tuple-element.813) | copy-start | bytes 52
  322.3 368.4 %all-gather.17.cloned.1.call-start = ((), (), s32[]{:S(2)}) async-start(), calls=%async_computation.20 | async-start | bytes 13369344 | tf_op jit(solution)/shard_map/all_gather | solution.py:171
  322.8 380.1 %all-gather.19.cloned.1.call-start = ((), (), s32[]{:S(2)}) async-start(), calls=%async_computation.21 | async-start | bytes 13369344 | tf_op jit(solution)/shard_map/all_gather | solution.py:172
  323.6 543.8 %all-reduce.22.cloned.1.call-start = ((), (), s32[]{:S(2)}) async-start(), calls=%async_computation.23 | async-start | bytes 8388608 | tf_op jit(solution)/shard_map/psum | solution.py:190
  323.6 18.1 collective-permute-start
  341.7 115.0 %copy-start.17 = (bf16[128,3072]{1,0:T(8,128)(2,1)}, bf16[128,3072]{1,0:T(8,128)(2,1)S(1)}, u32[]{:S(2)}) copy-start(bf16[128,3072]{1,0:T(8,128)(2,1)S(1)} %collective-permute-done) | copy-start | bytes 2359300
  341.8 71.4 %collective-permute-start.1 = (bf16[256,3072]{1,0:T(8,128)(2,1)S(1)}, bf16[256,3072]{1,0:T(8,128)(2,1)S(1)}, u32[]{:S(2)}, u32[]{:S(2)}) collective-permute-start(bf16[256,3072]{1,0:T(8,128)(2,1)S(1)} %pad_maximum_fusion.2), channel_id=1, source_target_pairs={{0,28},{2,30},{4,0},{6,2},{8,4},{10,6},{12,8},{14,10},{16,12},{18,... | collective-permute-start | bytes 4718600 | tf_op jit(solution)/shard_map/ppermute | solution.py:17
  413.2 47.1 %copy-start.14 = (bf16[256,3072]{1,0:T(8,128)(2,1)}, bf16[256,3072]{1,0:T(8,128)(2,1)S(1)}, u32[]{:S(2)}) copy-start(bf16[256,3072]{1,0:T(8,128)(2,1)S(1)} %collective-permute-done.1) | copy-start | bytes 4718596
  413.4 48.1 %copy-start.61 = (bf16[128]{0:T(256)(128)(2,1)S(1)}, bf16[128]{0:T(256)(128)(2,1)}, u32[]{:S(2)}) copy-start(bf16[128]{0:T(256)(128)(2,1)} %param.32) | copy-start | bytes 772
  413.4 43.3 %collective-permute-start.2 = (bf16[512,3072]{1,0:T(8,128)(2,1)S(1)}, bf16[512,3072]{1,0:T(8,128)(2,1)S(1)}, u32[]{:S(2)}, u32[]{:S(2)}) collective-permute-start(bf16[512,3072]{1,0:T(8,128)(2,1)S(1)} %pad_maximum_fusion.1), channel_id=1, source_target_pairs={{0,24},{2,26},{4,28},{6,30},{8,0},{10,2},{12,4},{14,6},{16,8},{18,... | collective-permute-start | bytes 9437192 | tf_op jit(solution)/shard_map/ppermute | solution.py:17
  460.3 206.9 %collective-permute-start.3 = (bf16[1024,3072]{1,0:T(8,128)(2,1)}, bf16[1024,3072]{1,0:T(8,128)(2,1)}, u32[]{:S(2)}, u32[]{:S(2)}) collective-permute-start(bf16[1024,3072]{1,0:T(8,128)(2,1)} %pad_maximum_fusion), channel_id=1, source_target_pairs={{0,16},{2,18},{4,20},{6,22},{8,24},{10,26},{12,28},{14,30},{16,0},... | collective-permute-start | bytes 18874376 | tf_op jit(solution)/shard_map/ppermute | solution.py:17
  512.5 161.6 %copy-start.18 = (bf16[128,3072]{1,0:T(8,128)(2,1)S(1)}, bf16[128,3072]{1,0:T(8,128)(2,1)}, u32[]{:S(2)}) copy-start(bf16[128,3072]{1,0:T(8,128)(2,1)} %copy-done.17) | copy-start | bytes 2359300
  758.3 175.0 %all-reduce.20.cloned.1.call-start = ((), (), s32[]{:S(2)}) async-start(), calls=%async_computation.22 | async-start | bytes 4194304 | tf_op jit(solution)/shard_map/psum | solution.py:183
  941.7 33.9 %copy-start.20 = (bf16[2048,1,128]{2,0,1:T(8,128)(2,1)S(1)}, bf16[2048,1,128]{2,0,1:T(8,128)(2,1)}, u32[]{:S(2)}) copy-start(bf16[2048,1,128]{2,0,1:T(8,128)(2,1)} %copy-done.19) | copy-start | bytes 1572868
  941.7 33.9 %copy-start.22 = (bf16[2048,1,128]{2,0,1:T(8,128)(2,1)S(1)}, bf16[2048,1,128]{2,0,1:T(8,128)(2,1)}, u32[]{:S(2)}) copy-start(bf16[2048,1,128]{2,0,1:T(8,128)(2,1)} %copy-done.21) | copy-start | bytes 1572868
  941.7 33.9 %copy-start.37 = (s32[2048]{0:T(1024)S(1)}, s32[2048]{0:T(1024)}, u32[]{:S(2)}) copy-start(s32[2048]{0:T(1024)} %param.22) | copy-start | bytes 24580
  942.9 30.6 %all-to-all-start.4 = ((bf16[512,8,128]{2,0,1:T(8,128)(2,1)}), bf16[512,8,128]{2,0,1:T(8,128)(2,1)S(1)}, u32[]{:S(2)}, u32[]{:S(2)}) async-start(bf16[512,8,128]{2,0,1:T(8,128)(2,1)} %bitcast.301), calls=%async_computation.4 | async-start | bytes 2097152 | tf_op jit(solution)/shard_map/all_to_all | solution.py:200
  1098.9 17.5 all-to-all-start.6
  1116.4 18.4 all-to-all-start.7
  1134.8 29.6 %all-to-all-start.5 = ((bf16[2048,2,128]{2,1,0:T(2,128)(2,1)}), bf16[2048,2,128]{2,1,0:T(2,128)(2,1)}, u32[]{:S(2)}, u32[]{:S(2)}) async-start(bf16[2048,2,128]{2,1,0:T(2,128)(2,1)} %copy.191), calls=%async_computation.5 | async-start | bytes 2097152 | tf_op jit(solution)/shard_map/all_to_all | solution.py:233
  1139.1 147.9 %all-reduce.24.cloned.1.call-start = ((), (), s32[]{:S(2)}) async-start(), calls=%async_computation.24 | async-start | bytes 8388608 | tf_op jit(solution)/shard_map/psum | solution.py:249
  1180.8 353.9 %reduce-scatter.20.cloned.1.call-start = ((), (), s32[]{:S(2)}) async-start(), calls=%async_computation.31 | async-start | bytes 26738688 | tf_op jit(solution)/shard_map/reduce_scatter | solution.py:276
  1196.5 414.3 %reduce-scatter.10.cloned.1.call-start = ((), (), s32[]{:S(2)}) async-start(), calls=%async_computation.26 | async-start | bytes 4456448 | tf_op jit(solution)/shard_map/reduce_scatter | solution.py:260
  1201.7 485.5 %reduce-scatter.12.cloned.1.call-start = ((), (), s32[]{:S(2)}) async-start(), calls=%async_computation.27 | async-start | bytes 4456448 | tf_op jit(solution)/shard_map/reduce_scatter | solution.py:263
  1205.2 589.0 %reduce-scatter.14.cloned.1.call-start = ((), (), s32[]{:S(2)}) async-start(), calls=%async_computation.28 | async-start | bytes 8912896 | tf_op jit(solution)/shard_map/reduce_scatter | solution.py:266
  1214.4 687.4 %reduce-scatter.8.cloned.1.call-start = ((), (), s32[]{:S(2)}) async-start(), calls=%async_computation.25 | async-start | bytes 8912896 | tf_op jit(solution)/shard_map/reduce_scatter | solution.py:257
  1221.6 928.0 %reduce-scatter.16.cloned.1.call-start = ((), (), s32[]{:S(2)}) async-start(), calls=%async_computation.29 | async-start | bytes 26738688 | tf_op jit(solution)/shard_map/reduce_scatter | solution.py:270
  1235.9 1160.8 %reduce-scatter.18.cloned.1.call-start = ((), (), s32[]{:S(2)}) async-start(), calls=%async_computation.30 | async-start | bytes 26738688 | tf_op jit(solution)/shard_map/reduce_scatter | solution.py:273
  1250.2 40.3 %copy-start.54 = (f32[2048]{0:T(1024)S(1)}, f32[2048]{0:T(1024)}, u32[]{:S(2)}) copy-start(f32[2048]{0:T(1024)} %get-tuple-element.389) | copy-start | bytes 24580
  1250.2 110.5 %copy-start.56 = (f32[512]{0:T(512)S(1)}, f32[512]{0:T(512)}, u32[]{:S(2)}) copy-start(f32[512]{0:T(512)} %copy-done.55) | copy-start | bytes 6148
  (52 other events, 289.6 us)
Sparse Core Ops, SparseCore 0:
  10.2 44.3 all-gather.10
  56.8 41.7 all-gather.12
  100.9 47.9 all-gather.8
  182.4 57.7 all-gather.14
  322.4 106.0 all-reduce.17
  430.7 134.3 all-gather.16
  567.4 126.9 all-gather.18
  758.4 108.9 all-reduce.21
  870.3 62.9 all-reduce.19
  1180.9 106.0 all-reduce.23
  1291.1 243.4 reduce-scatter.19
  1538.9 71.8 reduce-scatter.9
  1615.3 71.8 reduce-scatter.11
  1691.7 102.4 reduce-scatter.13
  1798.7 103.0 reduce-scatter.7
  1906.3 243.1 reduce-scatter.15
  2154.1 242.6 reduce-scatter.17
